TPU v7x, 32 devices: a whole 2x2x4 slice. The times are simulated.
32 devices in a mesh: seq: 4 (over z), shard: 8 (over y, x, core).
Axes of the slice: x: 2, y: 2, z: 4, core: 2. Of those that a mesh axis runs over, the one named last changes fastest.
Arguments:
- tokens: bfloat16 [2, 8, 2048, 768], P(None, 'shard', 'seq'), may hold values from -6 to 6
- lengths: int32 [8, 2], P('shard'), may hold values from 512 to 2048, as said below
- w_qkv: bfloat16 [768, 2304], P('shard'), may hold values from -0.21875 to 0.21875
- b_query: bfloat16 [768], P('shard'), may hold values from -3 to 3
- b_value: bfloat16 [768], P('shard'), may hold values from -3 to 3
- w_out: bfloat16 [768, 768], P('shard'), may hold values from -6 to 6
- b_out: bfloat16 [768], P('shard'), may hold values from -3 to 3
- gain_one: bfloat16 [768], P('shard'), may hold values from 0.5 to 1.5
- shift_one: bfloat16 [768], P('shard'), may hold values from -3 to 3
- w_up: bfloat16 [768, 3072], P('shard'), may hold values from -0.21875 to 0.21875
- b_up: bfloat16 [3072], P('shard'), may hold values from -3 to 3
- w_down: bfloat16 [3072, 768], P('shard'), may hold values from -0.109375 to 0.109375
- b_down: bfloat16 [768], P('shard'), may hold values from -3 to 3
- gain_two: bfloat16 [768], P('shard'), may hold values from 0.5 to 1.5
- shift_two: bfloat16 [768], P('shard'), may hold values from -3 to 3
- cotangent: bfloat16 [2, 8, 2048, 768], P(None, 'shard', 'seq'), may hold values from -6 to 6
Outputs:
- layer_out: bfloat16 [2, 8, 2048, 768], P(None, 'shard', 'seq')
- input_grad: bfloat16 [2, 8, 2048, 768], P(None, 'shard', 'seq')
- grad_w_qkv: float32 [768, 2304], P('shard')
- grad_b_query: float32 [768], P('shard')
- grad_b_value: float32 [768], P('shard')
- grad_w_out: float32 [768, 768], P('shard')
- grad_b_out: float32 [768], P('shard')
- grad_gain_one: float32 [768], P('shard')
- grad_shift_one: float32 [768], P('shard')
- grad_w_up: float32 [768, 3072], P('shard')
- grad_b_up: float32 [3072], P('shard')
- grad_w_down: float32 [3072, 768], P('shard')
- grad_b_down: float32 [768], P('shard')
- grad_gain_two: float32 [768], P('shard')
- grad_shift_two: float32 [768], P('shard')
Inputs may be any that keep to these rules, and one draw needn't show every extreme that they name: `lengths`: each group's sequence in each micro-batch has this many valid tokens at the start of its 2048 slots; some entry equals 2048.
All inputs are finite; a program needn't handle non-finite values.
Results may differ from a plain program's by a relative error of at most 0.015.
Values may be sent and summed in bfloat16 or wider, within the bound.
A program may use at most 192 MiB of HBM per device.

v0:
```python
import math
import jax
import jax.numpy as jnp
from jax import lax
from jax.sharding import PartitionSpec as P

H = 12
norm_eps = 1e-06


def layer_norm(inputs, scales, shifts):
    centre = jnp.mean(inputs, axis=-1, keepdims=True)
    centred = inputs - centre
    spread = jnp.mean(centred * centred, axis=-1, keepdims=True)
    return centred * lax.rsqrt(spread + norm_eps) * scales + shifts


def gelu_exact(inputs):
    return jax.nn.gelu(inputs, approximate=False)


def matmul_plain(left, right):
    return jnp.dot(left, right, preferred_element_type=jnp.float32)


def matmul_left_t(left, right):
    return lax.dot_general(
        left, right, (((0,), (0,)), ((), ())), preferred_element_type=jnp.float32
    )


def matmul_right_t(left, right):
    return lax.dot_general(
        left, right, (((1,), (1,)), ((), ())), preferred_element_type=jnp.float32
    )


def fetch_forward(
    w_qkv,
    b_query,
    b_value,
    w_out,
    b_out,
    gain_one,
    shift_one,
    w_up,
    b_up,
    w_down,
    b_down,
    gain_two,
    shift_two,
):
    return (
        lax.all_gather(w_qkv, "shard", axis=0, tiled=True),
        lax.all_gather(b_query, "shard", axis=0, tiled=True),
        lax.all_gather(b_value, "shard", axis=0, tiled=True),
        lax.all_gather(w_out, "shard", axis=0, tiled=True),
        lax.all_gather(b_out, "shard", axis=0, tiled=True),
        lax.all_gather(gain_one, "shard", axis=0, tiled=True),
        lax.all_gather(shift_one, "shard", axis=0, tiled=True),
        lax.all_gather(w_up, "shard", axis=0, tiled=True),
        lax.all_gather(b_up, "shard", axis=0, tiled=True),
        lax.all_gather(w_down, "shard", axis=0, tiled=True),
        lax.all_gather(b_down, "shard", axis=0, tiled=True),
        lax.all_gather(gain_two, "shard", axis=0, tiled=True),
        lax.all_gather(shift_two, "shard", axis=0, tiled=True),
    )


def fetch_backward(
    w_qkv,
    b_query,
    b_value,
    w_out,
    b_out,
    gain_one,
    shift_one,
    w_up,
    b_up,
    w_down,
    b_down,
    gain_two,
    shift_two,
):
    return (
        lax.all_gather(w_qkv, "shard", axis=0, tiled=True),
        lax.all_gather(b_query, "shard", axis=0, tiled=True),
        lax.all_gather(b_value, "shard", axis=0, tiled=True),
        lax.all_gather(w_out, "shard", axis=0, tiled=True),
        lax.all_gather(b_out, "shard", axis=0, tiled=True),
        lax.all_gather(gain_one, "shard", axis=0, tiled=True),
        lax.all_gather(shift_one, "shard", axis=0, tiled=True),
        lax.all_gather(w_up, "shard", axis=0, tiled=True),
        lax.all_gather(b_up, "shard", axis=0, tiled=True),
        lax.all_gather(w_down, "shard", axis=0, tiled=True),
        lax.all_gather(b_down, "shard", axis=0, tiled=True),
        lax.all_gather(gain_two, "shard", axis=0, tiled=True),
        lax.all_gather(shift_two, "shard", axis=0, tiled=True),
    )


def attention_forward(qkv_heads, seq_length):
    seq_slots, _, head_count, head_dim = qkv_heads.shape
    scaling = 1.0 / math.sqrt(head_dim)
    block_rows = min(512, seq_slots)
    queries = qkv_heads[:, 0].reshape(seq_slots // block_rows, block_rows, head_count, head_dim)
    key_rows = qkv_heads[:, 1]
    value_rows = qkv_heads[:, 2]
    key_valid = jnp.arange(seq_slots, dtype=jnp.int32) < seq_length

    def one_block(q_block):
        scores = (
            jnp.einsum("qhd,khd->hqk", q_block, key_rows, preferred_element_type=jnp.float32)
            * scaling
        )
        scores = jnp.where(key_valid[None, None, :], scores, -1e30)
        row_max = jnp.max(scores, axis=-1, keepdims=True)
        row_sum = jnp.sum(jnp.exp(scores - row_max), axis=-1, keepdims=True)
        log_total = row_max + jnp.log(row_sum)
        probs = jnp.exp(scores - log_total).astype(jnp.bfloat16)
        context = jnp.einsum("hqk,khd->qhd", probs, value_rows, preferred_element_type=jnp.float32)
        return (context.astype(jnp.bfloat16), log_total[..., 0])

    context, log_total = lax.map(one_block, queries)
    return (context.reshape(seq_slots, head_count * head_dim), log_total)


def attention_backward(qkv_heads, log_total, grad_context, seq_length):
    seq_slots, _, head_count, head_dim = qkv_heads.shape
    scaling = 1.0 / math.sqrt(head_dim)
    block_rows = min(512, seq_slots)
    block_count = seq_slots // block_rows
    queries = qkv_heads[:, 0].reshape(block_count, block_rows, head_count, head_dim)
    key_rows = qkv_heads[:, 1]
    value_rows = qkv_heads[:, 2]
    grad_blocks = grad_context.reshape(block_count, block_rows, head_count, head_dim)
    key_valid = jnp.arange(seq_slots, dtype=jnp.int32) < seq_length

    def one_block(carried, block_item):
        key_grad, value_grad = carried
        q_block, log_block, grad_block = block_item
        scores = (
            jnp.einsum("qhd,khd->hqk", q_block, key_rows, preferred_element_type=jnp.float32)
            * scaling
        )
        scores = jnp.where(key_valid[None, None, :], scores, -1e30)
        probs = jnp.exp(scores - log_block[..., None])
        grad_probs = jnp.einsum(
            "qhd,khd->hqk", grad_block, value_rows, preferred_element_type=jnp.float32
        )
        row_dot = jnp.sum(probs * grad_probs, axis=-1, keepdims=True)
        grad_scores = (probs * (grad_probs - row_dot)).astype(jnp.bfloat16)
        query_grad = (
            jnp.einsum("hqk,khd->qhd", grad_scores, key_rows, preferred_element_type=jnp.float32)
            * scaling
        )
        key_grad = (
            key_grad
            + jnp.einsum("hqk,qhd->khd", grad_scores, q_block, preferred_element_type=jnp.float32)
            * scaling
        )
        value_grad = value_grad + jnp.einsum(
            "hqk,qhd->khd",
            probs.astype(jnp.bfloat16),
            grad_block,
            preferred_element_type=jnp.float32,
        )
        return ((key_grad, value_grad), query_grad)

    zero_acc = jnp.zeros((seq_slots, head_count, head_dim), jnp.float32)
    (key_grad, value_grad), query_grad = lax.scan(
        one_block, (zero_acc, zero_acc), (queries, log_total, grad_blocks)
    )
    query_grad = query_grad.reshape(seq_slots, head_count, head_dim)
    return jnp.stack([query_grad, key_grad, value_grad], axis=1).astype(jnp.bfloat16)


def on_device(
    tokens,
    lengths,
    w_qkv,
    b_query,
    b_value,
    w_out,
    b_out,
    gain_one,
    shift_one,
    w_up,
    b_up,
    w_down,
    b_down,
    gain_two,
    shift_two,
    cotangent,
):
    micro_count = tokens.shape[0]
    tok_rows = tokens.shape[2]
    width = tokens.shape[3]
    seq_devices = lax.axis_size("seq")
    seq_place = lax.axis_index("seq")
    shard_count = lax.axis_size("shard")
    head_local = H // seq_devices
    head_dim = width // H
    seq_slots = tok_rows * seq_devices
    positions = seq_place * tok_rows + jnp.arange(tok_rows, dtype=jnp.int32)
    shards = (
        w_qkv,
        b_query,
        b_value,
        w_out,
        b_out,
        gain_one,
        shift_one,
        w_up,
        b_up,
        w_down,
        b_down,
        gain_two,
        shift_two,
    )
    grad_sums = [
        jnp.zeros((piece.shape[0] * shard_count,) + piece.shape[1:], jnp.float32)
        for piece in shards
    ]
    outputs = []
    input_grads = []
    for current in range(micro_count):
        weights_full = fetch_forward(*shards)
        (
            qkv_matrix,
            query_bias,
            value_bias,
            out_matrix,
            out_bias,
            gain_first,
            shift_first,
            up_matrix,
            up_bias,
            down_matrix,
            down_bias,
            gain_second,
            shift_second,
        ) = weights_full
        inputs_mb = tokens[current, 0]
        seq_length = lengths[0, current]
        row_valid = (positions < seq_length).astype(jnp.float32)[:, None]
        bias_all = jnp.concatenate([query_bias, jnp.zeros_like(query_bias), value_bias]).astype(
            jnp.float32
        )
        projected = (matmul_plain(inputs_mb, qkv_matrix) + bias_all).astype(jnp.bfloat16)
        qkv_heads = lax.all_to_all(
            projected.reshape(tok_rows, 3, seq_devices, head_local * head_dim),
            "seq",
            split_axis=2,
            concat_axis=0,
            tiled=True,
        )
        qkv_heads = qkv_heads.reshape(seq_slots, 3, head_local, head_dim)
        context_heads, log_total = attention_forward(qkv_heads, seq_length)
        context = lax.all_to_all(context_heads, "seq", split_axis=0, concat_axis=1, tiled=True)
        gain_first_f = gain_first.astype(jnp.float32)
        shift_first_f = shift_first.astype(jnp.float32)
        gain_second_f = gain_second.astype(jnp.float32)
        shift_second_f = shift_second.astype(jnp.float32)
        residual_one = (
            inputs_mb.astype(jnp.float32)
            + matmul_plain(context, out_matrix)
            + out_bias.astype(jnp.float32)
        )
        hidden_one = layer_norm(residual_one, gain_first_f, shift_first_f)
        hidden_low = hidden_one.astype(jnp.bfloat16)
        up_proj = matmul_plain(hidden_low, up_matrix) + up_bias.astype(jnp.float32)
        activated = gelu_exact(up_proj).astype(jnp.bfloat16)
        residual_two = (
            hidden_one + matmul_plain(activated, down_matrix) + down_bias.astype(jnp.float32)
        )
        outputs.append(layer_norm(residual_two, gain_second_f, shift_second_f).astype(jnp.bfloat16))
        weights_full = fetch_backward(*shards)
        (
            qkv_matrix,
            query_bias,
            value_bias,
            out_matrix,
            out_bias,
            gain_first,
            shift_first,
            up_matrix,
            up_bias,
            down_matrix,
            down_bias,
            gain_second,
            shift_second,
        ) = weights_full
        out_grad = cotangent[current, 0].astype(jnp.float32) * row_valid
        _, back_second = jax.vjp(layer_norm, residual_two, gain_second_f, shift_second_f)
        grad_residual_two, grad_gain_second, grad_shift_second = back_second(out_grad)
        down_grad = grad_residual_two.astype(jnp.bfloat16)
        grad_down = matmul_left_t(activated, down_grad)
        grad_down_bias = jnp.sum(down_grad.astype(jnp.float32), axis=0)
        _, back_gelu = jax.vjp(gelu_exact, up_proj)
        (grad_up_proj,) = back_gelu(matmul_right_t(down_grad, down_matrix))
        up_grad = grad_up_proj.astype(jnp.bfloat16)
        grad_up = matmul_left_t(hidden_low, up_grad)
        grad_up_bias = jnp.sum(up_grad.astype(jnp.float32), axis=0)
        grad_hidden_one = grad_residual_two + matmul_right_t(up_grad, up_matrix)
        _, back_first = jax.vjp(layer_norm, residual_one, gain_first_f, shift_first_f)
        grad_residual_one, grad_gain_first, grad_shift_first = back_first(grad_hidden_one)
        attn_grad = grad_residual_one.astype(jnp.bfloat16)
        grad_out = matmul_left_t(context, attn_grad)
        grad_out_bias = jnp.sum(attn_grad.astype(jnp.float32), axis=0)
        context_grad = matmul_right_t(attn_grad, out_matrix).astype(jnp.bfloat16)
        grad_heads = lax.all_to_all(context_grad, "seq", split_axis=1, concat_axis=0, tiled=True)
        grad_heads = grad_heads.reshape(seq_slots, head_local, head_dim)
        qkv_head_grad = attention_backward(qkv_heads, log_total, grad_heads, seq_length)
        qkv_grad = lax.all_to_all(
            qkv_head_grad.reshape(seq_slots, 3, 1, head_local * head_dim),
            "seq",
            split_axis=0,
            concat_axis=2,
            tiled=True,
        )
        qkv_grad = qkv_grad.reshape(tok_rows, 3 * width)
        grad_qkv = matmul_left_t(inputs_mb, qkv_grad)
        bias_grad_all = jnp.sum(qkv_grad.astype(jnp.float32), axis=0)
        input_grads.append(
            (grad_residual_one + matmul_right_t(qkv_grad, qkv_matrix)).astype(jnp.bfloat16)
        )
        terms = (
            grad_qkv,
            bias_grad_all[:width],
            bias_grad_all[2 * width :],
            grad_out,
            grad_out_bias,
            grad_gain_first,
            grad_shift_first,
            grad_up,
            grad_up_bias,
            grad_down,
            grad_down_bias,
            grad_gain_second,
            grad_shift_second,
        )
        grad_sums = [total + term for total, term in zip(grad_sums, terms)]
    shard_sums = (
        lax.psum_scatter(grad_sums[0], "shard", scatter_dimension=0, tiled=True),
        lax.psum_scatter(grad_sums[1], "shard", scatter_dimension=0, tiled=True),
        lax.psum_scatter(grad_sums[2], "shard", scatter_dimension=0, tiled=True),
        lax.psum_scatter(grad_sums[3], "shard", scatter_dimension=0, tiled=True),
        lax.psum_scatter(grad_sums[4], "shard", scatter_dimension=0, tiled=True),
        lax.psum_scatter(grad_sums[5], "shard", scatter_dimension=0, tiled=True),
        lax.psum_scatter(grad_sums[6], "shard", scatter_dimension=0, tiled=True),
        lax.psum_scatter(grad_sums[7], "shard", scatter_dimension=0, tiled=True),
        lax.psum_scatter(grad_sums[8], "shard", scatter_dimension=0, tiled=True),
        lax.psum_scatter(grad_sums[9], "shard", scatter_dimension=0, tiled=True),
        lax.psum_scatter(grad_sums[10], "shard", scatter_dimension=0, tiled=True),
        lax.psum_scatter(grad_sums[11], "shard", scatter_dimension=0, tiled=True),
        lax.psum_scatter(grad_sums[12], "shard", scatter_dimension=0, tiled=True),
    )
    summed = (
        lax.psum(shard_sums[0].astype(jnp.bfloat16), "seq").astype(jnp.float32),
        lax.psum(shard_sums[1].astype(jnp.bfloat16), "seq").astype(jnp.float32),
        lax.psum(shard_sums[2].astype(jnp.bfloat16), "seq").astype(jnp.float32),
        lax.psum(shard_sums[3].astype(jnp.bfloat16), "seq").astype(jnp.float32),
        lax.psum(shard_sums[4].astype(jnp.bfloat16), "seq").astype(jnp.float32),
        lax.psum(shard_sums[5].astype(jnp.bfloat16), "seq").astype(jnp.float32),
        lax.psum(shard_sums[6].astype(jnp.bfloat16), "seq").astype(jnp.float32),
        lax.psum(shard_sums[7].astype(jnp.bfloat16), "seq").astype(jnp.float32),
        lax.psum(shard_sums[8].astype(jnp.bfloat16), "seq").astype(jnp.float32),
        lax.psum(shard_sums[9].astype(jnp.bfloat16), "seq").astype(jnp.float32),
        lax.psum(shard_sums[10].astype(jnp.bfloat16), "seq").astype(jnp.float32),
        lax.psum(shard_sums[11].astype(jnp.bfloat16), "seq").astype(jnp.float32),
        lax.psum(shard_sums[12].astype(jnp.bfloat16), "seq").astype(jnp.float32),
    )
    layer_out = jnp.stack(outputs, axis=0)[:, None]
    input_grad = jnp.stack(input_grads, axis=0)[:, None]
    return (
        layer_out,
        input_grad,
        summed[0],
        summed[1],
        summed[2],
        summed[3],
        summed[4],
        summed[5],
        summed[6],
        summed[7],
        summed[8],
        summed[9],
        summed[10],
        summed[11],
        summed[12],
    )


def solution(mesh):
    placed = (
        P(None, "shard", "seq", None),
        P("shard", None),
        P("shard", None),
        P("shard"),
        P("shard"),
        P("shard", None),
        P("shard"),
        P("shard"),
        P("shard"),
        P("shard", None),
        P("shard"),
        P("shard", None),
        P("shard"),
        P("shard"),
        P("shard"),
        P(None, "shard", "seq", None),
    )
    return jax.shard_map(
        on_device,
        mesh=mesh,
        in_specs=placed,
        out_specs=(
            P(None, "shard", "seq", None),
            P(None, "shard", "seq", None),
            P("shard", None),
            P("shard"),
            P("shard"),
            P("shard", None),
            P("shard"),
            P("shard"),
            P("shard"),
            P("shard", None),
            P("shard"),
            P("shard", None),
            P("shard"),
            P("shard"),
            P("shard"),
        ),
        check_vma=False,
    )
```

profile of v0, /device:TPU:0, one launch (start us, length us, event | category | flops | bytes accessed | tf_op | source)
XLA Modules:
  0.0 961.6 jit_solution(3195086936663808667)
XLA Ops:
  16.6 27.1 %all-reduce.18 = (bf16[768]{0:T(1024)(128)(2,1)S(1)}, bf16[768]{0:T(1024)(128)(2,1)S(1)}, bf16[768]{0:T(1024)(128)(2,1)}, bf16[768]{0:T(1024)(128)(2,1)}, bf16[7...) all-reduce(bf16[768]{0:T(1024)(128)(2,1)S(1)} %dynamic-update-slice, ...), channel_id=1, replica_groups=mesh['seq'=4,'shard'=8] {'shard'}, use_global_device_ids=true, to_apply=%add.1 | all-reduce | flops 6144 | bytes 24576
  76.9 39.0 %all-to-all-done = bf16[512,3,4,192]{0,3,1,2:T(8,128)(2,1)S(1)} async-done(((bf16[512,3,4,192]{0,3,1,2:T(8,128)(2,1)}), bf16[512,3,4,192]{0,3,1,2:T(8,128)(2,1)S(1)}, u32[]{:S(2)}, u32[]{:S(2)}) %all-to-all-start) | async-done | bytes 2359328 | tf_op jit(solution)/shard_map/all_to_all | solution.py:251
  123.9 5.9 reshape.403
  133.3 36.4 %while.56 = (s32[]{:T(128)}, bf16[4,512,3,64]{1,3,2,0:T(8,128)(2,1)}, f32[4,3,512]{2,1,0:T(4,128)S(1)}, bf16[4,512,3,64]{1,3,2,0:T(8,128)(2,1)S(1)}, bf16[2048,3...) while((s32[]{:T(128)}, ...), condition=%wide.region_3.4_spmd.clone, body=%wide.region_0.3_spmd.clone.sunk | while | flops 840008192 | bytes 39780960 | solution.py:124
  183.8 5.9 reshape.405
  192.3 34.0 %while.57 = (s32[]{:T(128)}, bf16[4,512,3,64]{1,3,2,0:T(8,128)(2,1)S(1)}, f32[4,3,512]{2,1,0:T(4,128)S(1)}, bf16[4,512,3,64]{1,3,2,0:T(8,128)(2,1)S(1)}, bf16[20...) while((s32[]{:T(128)}, ...), condition=%wide.region_11.12_spmd.clone, body=%wide.region_8.11_spmd.clone.sunk | while | flops 840008192 | bytes 39782500 | solution.py:124
  232.9 8.8 all-gather
  262.9 34.8 %multiply_convert_fusion.3 = (bf16[512,3072]{1,0:T(8,128)(2,1)}, f32[512,3072]{1,0:T(8,128)}, bf16[512,3072]{1,0:T(8,128)(2,1)}, f32[512,3072]{1,0:T(8,128)}, f32[512,3072]{1,0:T(8,128)}) fusion(f32[3072]{0:T(1024)S(1)} %bitcast.336, f32[512,3072]{1,0:T(8,128)S(1)} %fusion.144, bf16[768,3072]{1,0:T(8,128)(2,1)S(1)} %copy-done.66, ...), kind=kOutput, calls=%fused_computation.126 | convolution fusion | flops 2625503232 | bytes 37771264 | tf_op jit(solution)/shard_map/dot_general | solution.py:23
  297.6 6.2 fusion.161
  320.2 18.1 %convert_reduce_fusion.1 = (f32[3072]{0:T(1024)}, bf16[512,3072]{1,0:T(8,128)(2,1)}, f32[3072]{0:T(1024)}, bf16[512,3072]{1,0:T(8,128)(2,1)}) fusion(f32[512,3072]{1,0:T(8,128)} %get-tuple-element.761, f32[512,3072]{1,0:T(8,128)} %get-tuple-element.802, f32[3072]{0:T(1024)S(1)} %bitcast.337, f32[512,3072]{1,0:T(8,128)} %fusion.162, ...), kind=kOutput, calls=%fused_computation.110 | convolution fusion | flops 2469390336 | bytes 43290624 | tf_op jit(solution)/shard_map/dot_general | solution.py:33
  338.3 6.1 add_add_fusion.8
  344.4 6.4 multiply_reduce_fusion.3
  380.0 9.0 fusion.146
  393.0 8.9 convolution_add_fusion.1
  408.2 124.5 %while.58 = (s32[]{:T(128)}, f32[2048,3,64]{0,2,1:T(8,128)S(1)}, f32[2048,3,64]{0,2,1:T(8,128)}, bf16[4,512,3,64]{1,3,2,0:T(8,128)(2,1)}, bf16[4,512,3,64]{1,3,2...) while((s32[]{:T(128)}, f32[2048,3,64]{0,2,1:T(8,128)S(1)}, ...), condition=%wide.region_22.23_spmd.clone, body=%wide.region_20.22_spmd.clone.sunk | while | flops 2062516736 | bytes 204919504 | solution.py:171
  427.4 7.0 fusion.273
  458.0 6.4 fusion.273
  488.6 7.4 fusion.273
  520.7 6.4 fusion.273
  548.5 120.6 %while.59 = (s32[]{:T(128)}, f32[2048,3,64]{0,2,1:T(8,128)S(1)}, f32[2048,3,64]{0,2,1:T(8,128)}, bf16[4,512,3,64]{1,3,2,0:T(8,128)(2,1)}, bf16[4,512,3,64]{1,3,2...) while((s32[]{:T(128)}, f32[2048,3,64]{0,2,1:T(8,128)S(1)}, ...), condition=%wide.region_29.30_spmd.clone, body=%wide.region_27.29_spmd.clone.sunk | while | flops 2062516736 | bytes 204919504 | solution.py:171
  567.1 6.3 fusion.286
  596.8 6.3 fusion.286
  627.1 6.3 fusion.286
  657.4 6.3 fusion.286
  683.3 7.8 copy.160
  691.1 81.0 %all-to-all-done.7 = bf16[2048,3,1,192]{3,1,2,0:T(4,128)(2,1)} async-done(((bf16[2048,3,1,192]{3,1,2,0:T(4,128)(2,1)}), bf16[2048,3,1,192]{3,1,2,0:T(4,128)(2,1)}, u32[]{:S(2)}, u32[]{:S(2)}) %all-to-all-start.7) | async-done | bytes 2359328 | tf_op jit(solution)/shard_map/all_to_all | solution.py:315
  772.1 7.2 copy.161
  791.1 8.0 copy.162
  812.9 50.6 %reduce-scatter.13.cloned.1.call-done = f32[96,2304]{1,0:T(8,128)} async-done(((f32[768,2304]{1,0:T(8,128)}), f32[96,2304]{1,0:T(8,128)}) %reduce-scatter.13.cloned.1.call-update) | async-done | bytes 884752
  867.2 24.6 %all-reduce.17 = (bf16[768]{0:T(1024)(128)(2,1)S(1)}, bf16[768]{0:T(1024)(128)(2,1)S(1)}, bf16[768]{0:T(1024)(128)(2,1)S(1)}, bf16[768]{0:T(1024)(128)(2,1)S(1)}...) all-reduce(f32[768]{0:T(1024)S(1)} %add.360, ...), channel_id=3, replica_groups=mesh['seq'=4,'shard'=8] {'shard'}, use_global_device_ids=true, to_apply=%region_34.35.clone | all-reduce | flops 9216 | bytes 55296
  892.5 12.8 %all-reduce.19 = (bf16[96]{0:T(256)(128)(2,1)S(1)}, bf16[96]{0:T(256)(128)(2,1)S(1)}, bf16[96]{0:T(256)(128)(2,1)S(1)}, bf16[96]{0:T(256)(128)(2,1)S(1)}, bf16[9...) all-reduce(bf16[96]{0:T(256)(128)(2,1)S(1)} %dynamic-slice.43, ...), channel_id=1, replica_groups=mesh['seq'=4,'shard'=8] {'seq'}, use_global_device_ids=true, to_apply=%region_35.36 | all-reduce | flops 1152 | bytes 4608 | tf_op jit(solution)/shard_map/psum | solution.py:361
  919.1 29.5 %all-reduce.23.cloned.1.call-done = (bf16[96,2304]{0,1:T(8,128)(2,1)}, bf16[96,768]{1,0:T(8,128)(2,1)}, bf16[96,3072]{1,0:T(8,128)(2,1)}, bf16[384,768]{1,0:T(8,128)(2,1)}) async-done(((bf16[96,2304]{0,1:T(8,128)(2,1)}, bf16[96,768]{1,0:T(8,128)(2,1)}, bf16[96,3072]{1,0:T(8,128)(2,1)}, bf16[384,768]{1,0:T(8,128)(2,1)}), (bf16[96,2304]{0,1:T(8,128)(2,1)}, bf16[96,768]{1,0:T(8,128)(2,1)}, ...) | async-done | bytes 1769488 | tf_op jit(solution)/shard_map/psum | solution.py:360
  (457 shorter events, 493.6 us)
Async XLA Ops:
  7.2 39.5 %all-gather.6.cloned.1.call-start = ((), (), s32[]{:S(2)}) async-start(), calls=%async_computation.12 | async-start | bytes 3981312 | tf_op jit(solution)/shard_map/all_gather | solution.py:54
  56.9 59.0 %all-to-all-start = ((bf16[512,3,4,192]{0,3,1,2:T(8,128)(2,1)}), bf16[512,3,4,192]{0,3,1,2:T(8,128)(2,1)S(1)}, u32[]{:S(2)}, u32[]{:S(2)}) async-start(bf16[512,3,4,192]{0,3,1,2:T(8,128)(2,1)} %copy.136), calls=%async_computation | async-start | bytes 4718592 | tf_op jit(solution)/shard_map/all_to_all | solution.py:251
  61.7 181.5 %all-gather.8.cloned.1.call-start = ((), (), s32[]{:S(2)}) async-start(), calls=%async_computation.13 | async-start | bytes 1327104 | tf_op jit(solution)/shard_map/all_gather | solution.py:57
  62.4 192.8 %all-gather.10.cloned.1.call-start = ((), (), s32[]{:S(2)}) async-start(), calls=%async_computation.14 | async-start | bytes 5308416 | tf_op jit(solution)/shard_map/all_gather | solution.py:61
  115.9 58.2 %all-to-all-start.2 = ((bf16[512,3,4,192]{0,3,1,2:T(8,128)(2,1)}), bf16[512,3,4,192]{0,3,1,2:T(8,128)(2,1)}, u32[]{:S(2)}, u32[]{:S(2)}) async-start(bf16[512,3,4,192]{0,3,1,2:T(8,128)(2,1)} %copy.140), calls=%async_computation.2 | async-start | bytes 4718592 | tf_op jit(solution)/shard_map/all_to_all | solution.py:251
  169.7 14.1 %copy-start.11 = (bf16[2048,3,64]{0,2,1:T(8,128)(2,1)}, bf16[2048,3,64]{0,2,1:T(8,128)(2,1)S(1)}, u32[]{:S(2)}) copy-start(bf16[2048,3,64]{0,2,1:T(8,128)(2,1)S(1)} %get-tuple-element.1187) | copy-start | bytes 2359300
  169.7 14.1 %copy-start.14 = (bf16[4,512,3,64]{1,3,2,0:T(8,128)(2,1)}, bf16[4,512,3,64]{1,3,2,0:T(8,128)(2,1)S(1)}, u32[]{:S(2)}) copy-start(bf16[4,512,3,64]{1,3,2,0:T(8,128)(2,1)S(1)} %get-tuple-element.1191) | copy-start | bytes 2359300
  169.7 14.1 %copy-start.37 = (f32[4,3,512]{2,1,0:T(4,128)}, f32[4,3,512]{2,1,0:T(4,128)S(1)}, u32[]{:S(2)}) copy-start(f32[4,3,512]{2,1,0:T(4,128)S(1)} %get-tuple-element.1134) | copy-start | bytes 73732
  174.1 52.2 %all-to-all-start.1 = ((bf16[4,512,192]{1,2,0:T(8,128)(2,1)}), bf16[4,512,192]{1,2,0:T(8,128)(2,1)}, u32[]{:S(2)}, u32[]{:S(2)}) async-start(bf16[4,512,192]{1,2,0:T(8,128)(2,1)} %bitcast.8), calls=%async_computation.1 | async-start | bytes 1572864 | tf_op jit(solution)/shard_map/all_to_all | solution.py:260
  192.2 40.6 %copy-start.63 = (bf16[768]{0:T(1024)(128)(2,1)S(1)}, bf16[768]{0:T(1024)(128)(2,1)}, u32[]{:S(2)}) copy-start(bf16[768]{0:T(1024)(128)(2,1)} %get-tuple-element.717) | copy-start | bytes 4612
  192.2 40.6 %copy-start.62 = (bf16[768]{0:T(1024)(128)(2,1)S(1)}, bf16[768]{0:T(1024)(128)(2,1)}, u32[]{:S(2)}) copy-start(bf16[768]{0:T(1024)(128)(2,1)} %get-tuple-element.719) | copy-start | bytes 4612
  192.3 40.6 %copy-start.61 = (bf16[768]{0:T(1024)(128)(2,1)S(1)}, bf16[768]{0:T(1024)(128)(2,1)}, u32[]{:S(2)}) copy-start(bf16[768]{0:T(1024)(128)(2,1)} %get-tuple-element.718) | copy-start | bytes 4612
  192.3 40.6 %copy-start.65 = (bf16[384]{0:T(512)(128)(2,1)S(1)}, bf16[384]{0:T(512)(128)(2,1)}, u32[]{:S(2)}) copy-start(bf16[384]{0:T(512)(128)(2,1)} %param.34) | copy-start | bytes 2308
  192.3 49.5 %copy-start.60 = (bf16[768]{0:T(1024)(128)(2,1)S(1)}, bf16[768]{0:T(1024)(128)(2,1)}, u32[]{:S(2)}) copy-start(bf16[768]{0:T(1024)(128)(2,1)} %get-tuple-element.720) | copy-start | bytes 4612
  192.3 49.5 %copy-start.59 = (bf16[768]{0:T(1024)(128)(2,1)S(1)}, bf16[768]{0:T(1024)(128)(2,1)}, u32[]{:S(2)}) copy-start(bf16[768]{0:T(1024)(128)(2,1)} %get-tuple-element.721) | copy-start | bytes 4612
  192.3 49.5 %copy-start.58 = (bf16[768]{0:T(1024)(128)(2,1)S(1)}, bf16[768]{0:T(1024)(128)(2,1)}, u32[]{:S(2)}) copy-start(bf16[768]{0:T(1024)(128)(2,1)} %get-tuple-element.722) | copy-start | bytes 4612
  226.3 20.7 %copy-start.4 = (bf16[2048,3,64]{0,2,1:T(8,128)(2,1)}, bf16[2048,3,64]{0,2,1:T(8,128)(2,1)S(1)}, u32[]{:S(2)}) copy-start(bf16[2048,3,64]{0,2,1:T(8,128)(2,1)S(1)} %get-tuple-element.1180) | copy-start | bytes 2359300
  226.3 20.7 %copy-start.9 = (bf16[2048,3,64]{0,2,1:T(8,128)(2,1)}, bf16[2048,3,64]{0,2,1:T(8,128)(2,1)S(1)}, u32[]{:S(2)}) copy-start(bf16[2048,3,64]{0,2,1:T(8,128)(2,1)S(1)} %get-tuple-element.1186) | copy-start | bytes 2359300
  226.3 20.7 %copy-start.13 = (bf16[4,512,3,64]{1,3,2,0:T(8,128)(2,1)}, bf16[4,512,3,64]{1,3,2,0:T(8,128)(2,1)S(1)}, u32[]{:S(2)}) copy-start(bf16[4,512,3,64]{1,3,2,0:T(8,128)(2,1)S(1)} %get-tuple-element.1190) | copy-start | bytes 2359300
  226.3 20.7 %copy-start.38 = (f32[4,3,512]{2,1,0:T(4,128)}, f32[4,3,512]{2,1,0:T(4,128)S(1)}, u32[]{:S(2)}) copy-start(f32[4,3,512]{2,1,0:T(4,128)S(1)} %get-tuple-element.1098) | copy-start | bytes 73732
  227.2 24.2 %all-to-all-start.3 = ((bf16[4,512,192]{1,2,0:T(8,128)(2,1)}), bf16[4,512,192]{1,2,0:T(8,128)(2,1)S(1)}, u32[]{:S(2)}, u32[]{:S(2)}) async-start(bf16[4,512,192]{1,2,0:T(8,128)(2,1)} %bitcast.331), calls=%async_computation.3 | async-start | bytes 1572864 | tf_op jit(solution)/shard_map/all_to_all | solution.py:260
  232.2 65.4 %all-gather.12.cloned.1.call-start = ((), (), s32[]{:S(2)}) async-start(), calls=%async_computation.15 | async-start | bytes 5308416 | tf_op jit(solution)/shard_map/all_gather | solution.py:63
  232.8 570.6 %reduce-scatter.7.cloned.1.call-start = ((), (), s32[]{:S(2)}) async-start(), calls=%async_computation.16 | async-start | bytes 2654208 | tf_op jit(solution)/shard_map/reduce_scatter | solution.py:348
  359.9 448.4 %reduce-scatter.11.cloned.1.call-start = ((), (), s32[]{:S(2)}) async-start(), calls=%async_computation.18 | async-start | bytes 10616832 | tf_op jit(solution)/shard_map/reduce_scatter | solution.py:354
  375.7 26.2 %all-to-all-start.4 = ((bf16[512,4,192]{0,2,1:T(8,128)(2,1)}), bf16[512,4,192]{0,2,1:T(8,128)(2,1)}, u32[]{:S(2)}, u32[]{:S(2)}) async-start(bf16[512,4,192]{0,2,1:T(8,128)(2,1)} %bitcast.330), calls=%async_computation.4 | async-start | bytes 1572864 | tf_op jit(solution)/shard_map/all_to_all | solution.py:312
  379.9 430.7 %reduce-scatter.9.cloned.1.call-start = ((), (), s32[]{:S(2)}) async-start(), calls=%async_computation.17 | async-start | bytes 10616832 | tf_op jit(solution)/shard_map/reduce_scatter | solution.py:352
  401.9 139.8 %all-to-all-start.6 = ((bf16[512,4,192]{0,2,1:T(8,128)(2,1)}), bf16[512,4,192]{0,2,1:T(8,128)(2,1)}, u32[]{:S(2)}, u32[]{:S(2)}) async-start(bf16[512,4,192]{0,2,1:T(8,128)(2,1)} %bitcast.329), calls=%async_computation.6 | async-start | bytes 1572864 | tf_op jit(solution)/shard_map/all_to_all | solution.py:312
  541.7 136.4 %all-to-all-start.5 = ((bf16[2048,3,1,192]{3,1,2,0:T(4,128)(2,1)}), bf16[2048,3,1,192]{3,1,2,0:T(4,128)(2,1)}, u32[]{:S(2)}, u32[]{:S(2)}) async-start(bf16[2048,3,1,192]{3,1,2,0:T(4,128)(2,1)} %copy.146), calls=%async_computation.5 | async-start | bytes 8388608 | tf_op jit(solution)/shard_map/all_to_all | solution.py:315
  678.1 94.0 %all-to-all-start.7 = ((bf16[2048,3,1,192]{3,1,2,0:T(4,128)(2,1)}), bf16[2048,3,1,192]{3,1,2,0:T(4,128)(2,1)}, u32[]{:S(2)}, u32[]{:S(2)}) async-start(bf16[2048,3,1,192]{3,1,2,0:T(4,128)(2,1)} %copy.152), calls=%async_computation.7 | async-start | bytes 8388608 | tf_op jit(solution)/shard_map/all_to_all | solution.py:315
  683.3 180.2 %reduce-scatter.13.cloned.1.call-start = ((), (), s32[]{:S(2)}) async-start(), calls=%async_computation.19 | async-start | bytes 7962624
  799.3 149.2 %all-reduce.23.cloned.1.call-start = ((), (), s32[]{:S(2)}) async-start(), calls=%async_computation.20 | async-start | bytes 3833856 | tf_op jit(solution)/shard_map/psum | solution.py:360
  812.9 97.1 %copy-start.53 = (f32[512]{0:T(512)S(1)}, f32[512]{0:T(512)}, u32[]{:S(2)}) copy-start(f32[512]{0:T(512)} %copy-done.52) | copy-start | bytes 6148
  (70 other events, 359.6 us)
Sparse Core Ops, SparseCore 0:
  9.9 36.7 all-gather.5
  64.4 24.3 all-gather.7
  90.7 38.7 all-gather.9
  234.6 39.2 all-gather.11
  360.0 40.3 reduce-scatter.6
  403.8 76.8 reduce-scatter.10
  484.1 76.8 reduce-scatter.8
  799.4 64.0 reduce-scatter.12
  867.3 81.2 all-reduce.22
where the time goes:
time: 971 us; the launch traced here: 962 us
  matrix products  389 us (40%)
  waiting for transfers between devices  215 us (22%)
  other arithmetic  115 us (12%)
  local copies, waits for them, and re-layouts  112 us (12%)
  blocking collectives  73.4 us (8%)
  starting transfers between devices  40 us (4%)
  between operations  17.3 us (2%)
    all_to_all x2, waiting for transfers between devices, on_device(): lax.all_to_all(qkv_head_grad.reshape(seq_slots, 3, 1, head_local * head_d...  81 us
    dot_general x8, matrix products, matmul_plain(): return jnp.dot(left, right, preferred_element_type=jnp.float32)  66.5 us
    unnamed x10, waiting for transfers between devices  53.3 us
    dot_general x8, matrix products, one_block(): jnp.einsum('hqk,khd->qhd', grad_scores, key_rows, preferred_element_type=...  52.3 us
    unnamed x2, blocking collectives  51.8 us
    dot_general x8, matrix products, matmul_right_t(): lax.dot_general(left, right, (((1,), (1,)), ((), ())), preferred_element_...  47.5 us
    all_to_all x2, waiting for transfers between devices, on_device(): lax.all_to_all(projected.reshape(tok_rows, 3, seq_devices, head_local * h...  43.5 us
    dot_general x8, matrix products, one_block(): jnp.einsum('hqk,qhd->khd', probs.astype(jnp.bfloat16), grad_block, prefer...  43.4 us
  transfers between devices with their start and end apart: 17, of which 7 were waited for; matrix products, arithmetic and copies ran while one was open for 55% of the time, Pallas kernels for 0%

commit v1 on v0

--- a/solution.py
+++ b/solution.py
@@ -312,12 +312,10 @@
         grad_heads = lax.all_to_all(context_grad, "seq", split_axis=1, concat_axis=0, tiled=True)
         grad_heads = grad_heads.reshape(seq_slots, head_local, head_dim)
         qkv_head_grad = attention_backward(qkv_heads, log_total, grad_heads, seq_length)
-        qkv_grad = lax.all_to_all(
-            qkv_head_grad.reshape(seq_slots, 3, 1, head_local * head_dim),
-            "seq",
-            split_axis=0,
-            concat_axis=2,
-            tiled=True,
+        arr = qkv_head_grad.reshape(seq_slots, 3, 1, head_local * head_dim)
+        qkv_grad = jnp.concatenate(
+            lax.all_to_all(jnp.stack(jnp.split(arr, lax.axis_size("seq"), axis=0)), "seq", 0, 0),
+            axis=2,
         )
         qkv_grad = qkv_grad.reshape(tok_rows, 3 * width)
         grad_qkv = matmul_left_t(inputs_mb, qkv_grad)

time: 971 us -> 916 us (0.943)
  waiting for transfers between devices: 215 us -> 181 us
  local copies, waits for them, and re-layouts: 112 us -> 89.6 us
    all_to_all x2, waiting for transfers between devices: 81 us -> 45.5 us  [on_device(): lax.all_to_all(jnp.stack(jnp.split(arr, lax.axis_size('seq'), axis=0)), '...]
    all_to_all x4 -> x2, local copies, waits for them, and re-layouts: 17.7 us -> 3.57 us  [on_device(): lax.all_to_all(jnp.stack(jnp.split(arr, lax.axis_size('seq'), axis=0)), '...]
  transfers between devices with their start and end apart: 17 -> 17, of which waited for: 7 -> 7; matrix products, arithmetic and copies ran while one was open for 55% -> 56% of each run, Pallas kernels for 0% -> 0%
where the time goes in v1:
time: 916 us; the launch traced here: 907 us
  matrix products  389 us (42%)
  waiting for transfers between devices  181 us (20%)
  other arithmetic  117 us (13%)
  local copies, waits for them, and re-layouts  89.6 us (10%)
  blocking collectives  73.3 us (8%)
  starting transfers between devices  40 us (4%)
  between operations  17.5 us (2%)
    dot_general x8, matrix products, matmul_plain(): return jnp.dot(left, right, preferred_element_type=jnp.float32)  66.5 us
    unnamed x10, waiting for transfers between devices  53.7 us
    dot_general x8, matrix products, one_block(): jnp.einsum('hqk,khd->qhd', grad_scores, key_rows, preferred_element_type=...  52.1 us
    unnamed x2, blocking collectives  51.4 us
    dot_general x8, matrix products, matmul_right_t(): lax.dot_general(left, right, (((1,), (1,)), ((), ())), preferred_element_...  47.6 us
    all_to_all x2, waiting for transfers between devices, on_device(): lax.all_to_all(jnp.stack(jnp.split(arr, lax.axis_size('seq'), axis=0)), '...  45.5 us
    dot_general x8, matrix products, one_block(): jnp.einsum('hqk,qhd->khd', probs.astype(jnp.bfloat16), grad_block, prefer...  43.8 us
    all_to_all x2, waiting for transfers between devices, on_device(): lax.all_to_all(projected.reshape(tok_rows, 3, seq_devices, head_local * h...  43.4 us
  transfers between devices with their start and end apart: 17, of which 7 were waited for; matrix products, arithmetic and copies ran while one was open for 56% of the time, Pallas kernels for 0%

profile of v1, /device:TPU:0, one launch (start us, length us, event | category | flops | bytes accessed | tf_op | source)
XLA Modules:
  0.0 907.4 jit_solution(18021644476392049747)
XLA Ops:
  16.6 27.2 %all-reduce.18 = (bf16[768]{0:T(1024)(128)(2,1)S(1)}, bf16[768]{0:T(1024)(128)(2,1)S(1)}, bf16[768]{0:T(1024)(128)(2,1)}, bf16[768]{0:T(1024)(128)(2,1)}, bf16[7...) all-reduce(bf16[768]{0:T(1024)(128)(2,1)S(1)} %dynamic-update-slice, ...), channel_id=1, replica_groups=mesh['seq'=4,'shard'=8] {'shard'}, use_global_device_ids=true, to_apply=%add.1 | all-reduce | flops 6144 | bytes 24576
  76.9 39.0 %all-to-all-done = bf16[512,3,4,192]{0,3,1,2:T(8,128)(2,1)S(1)} async-done(((bf16[512,3,4,192]{0,3,1,2:T(8,128)(2,1)}), bf16[512,3,4,192]{0,3,1,2:T(8,128)(2,1)S(1)}, u32[]{:S(2)}, u32[]{:S(2)}) %all-to-all-start) | async-done | bytes 2359328 | tf_op jit(solution)/shard_map/all_to_all | solution.py:251
  123.9 5.9 reshape.321
  133.2 36.4 %while.56 = (s32[]{:T(128)}, bf16[4,512,3,64]{1,3,2,0:T(8,128)(2,1)}, f32[4,3,512]{2,1,0:T(4,128)S(1)}, bf16[4,512,3,64]{1,3,2,0:T(8,128)(2,1)S(1)}, bf16[2048,3...) while((s32[]{:T(128)}, ...), condition=%wide.region_3.4_spmd.clone, body=%wide.region_0.3_spmd.clone.sunk | while | flops 840008192 | bytes 39780960 | solution.py:124
  183.6 5.9 reshape.323
  192.1 34.0 %while.57 = (s32[]{:T(128)}, bf16[4,512,3,64]{1,3,2,0:T(8,128)(2,1)S(1)}, f32[4,3,512]{2,1,0:T(4,128)S(1)}, bf16[4,512,3,64]{1,3,2,0:T(8,128)(2,1)S(1)}, bf16[20...) while((s32[]{:T(128)}, ...), condition=%wide.region_11.12_spmd.clone, body=%wide.region_8.11_spmd.clone.sunk | while | flops 840008192 | bytes 39782500 | solution.py:124
  232.7 8.8 all-gather
  262.7 34.8 %multiply_convert_fusion.3 = (bf16[512,3072]{1,0:T(8,128)(2,1)}, f32[512,3072]{1,0:T(8,128)}, bf16[512,3072]{1,0:T(8,128)(2,1)}, f32[512,3072]{1,0:T(8,128)}, f32[512,3072]{1,0:T(8,128)}) fusion(f32[3072]{0:T(1024)S(1)} %bitcast.350, f32[512,3072]{1,0:T(8,128)S(1)} %fusion.144, bf16[768,3072]{1,0:T(8,128)(2,1)S(1)} %copy-done.66, ...), kind=kOutput, calls=%fused_computation.126 | convolution fusion | flops 2625503232 | bytes 37771264 | tf_op jit(solution)/shard_map/dot_general | solution.py:23
  297.5 6.2 fusion.163
  320.1 18.1 %convert_reduce_fusion.1 = (f32[3072]{0:T(1024)}, bf16[512,3072]{1,0:T(8,128)(2,1)}, f32[3072]{0:T(1024)}, bf16[512,3072]{1,0:T(8,128)(2,1)}) fusion(f32[512,3072]{1,0:T(8,128)} %get-tuple-element.614, f32[512,3072]{1,0:T(8,128)} %get-tuple-element.663, f32[3072]{0:T(1024)S(1)} %bitcast.351, f32[512,3072]{1,0:T(8,128)} %fusion.164, ...), kind=kOutput, calls=%fused_computation.110 | convolution fusion | flops 2469390336 | bytes 43290624 | tf_op jit(solution)/shard_map/dot_general | solution.py:33
  338.3 6.1 add_add_fusion.8
  344.4 6.4 multiply_reduce_fusion.3
  379.8 9.0 fusion.146
  392.9 8.9 convolution_add_fusion.1
  408.1 124.4 %while.58 = (s32[]{:T(128)}, f32[2048,3,64]{0,2,1:T(8,128)S(1)}, f32[2048,3,64]{0,2,1:T(8,128)}, bf16[4,512,3,64]{1,3,2,0:T(8,128)(2,1)}, bf16[4,512,3,64]{1,3,2...) while((s32[]{:T(128)}, f32[2048,3,64]{0,2,1:T(8,128)S(1)}, ...), condition=%wide.region_22.23_spmd.clone, body=%wide.region_20.22_spmd.clone.sunk | while | flops 2062516736 | bytes 204919504 | solution.py:171
  427.3 7.0 fusion.275
  457.8 6.4 fusion.275
  488.4 7.4 fusion.275
  495.8 5.9 fusion.274
  520.5 6.4 fusion.275
  538.8 6.0 all-to-all-start.5
  545.7 120.8 %while.59 = (s32[]{:T(128)}, f32[2048,3,64]{0,2,1:T(8,128)S(1)}, f32[2048,3,64]{0,2,1:T(8,128)}, bf16[4,512,3,64]{1,3,2,0:T(8,128)(2,1)}, bf16[4,512,3,64]{1,3,2...) while((s32[]{:T(128)}, f32[2048,3,64]{0,2,1:T(8,128)S(1)}, ...), condition=%wide.region_29.30_spmd.clone, body=%wide.region_27.29_spmd.clone.sunk | while | flops 2062516736 | bytes 204919504 | solution.py:171
  564.3 6.2 fusion.288
  594.0 6.3 fusion.288
  624.4 6.2 fusion.288
  654.7 6.3 fusion.288
  681.3 45.5 %all-to-all-done.7 = bf16[4,512,3,1,192]{1,4,2,3,0:T(8,128)(2,1)S(1)} async-done(((bf16[4,512,3,1,192]{1,4,2,3,0:T(8,128)(2,1)}), bf16[4,512,3,1,192]{1,4,2,3,0:T(8,128)(2,1)S(1)}, u32[]{:S(2)}, u32[]{:S(2)}) %all-to-all-start.7) | async-done | bytes 2359328 | tf_op jit(solution)/shard_map/all_to_all | solution.py:317
  736.9 8.0 copy.101
  758.1 51.0 %reduce-scatter.13.cloned.1.call-done = f32[96,2304]{1,0:T(8,128)} async-done(((f32[768,2304]{1,0:T(8,128)}), f32[96,2304]{1,0:T(8,128)}) %reduce-scatter.13.cloned.1.call-update) | async-done | bytes 884752
  812.0 24.3 %all-reduce.17 = (bf16[768]{0:T(1024)(128)(2,1)S(1)}, bf16[768]{0:T(1024)(128)(2,1)S(1)}, bf16[768]{0:T(1024)(128)(2,1)S(1)}, bf16[768]{0:T(1024)(128)(2,1)S(1)}...) all-reduce(f32[768]{0:T(1024)S(1)} %add.360, ...), channel_id=3, replica_groups=mesh['seq'=4,'shard'=8] {'shard'}, use_global_device_ids=true, to_apply=%region_34.35.clone | all-reduce | flops 9216 | bytes 55296
  837.0 13.0 %all-reduce.19 = (bf16[96]{0:T(256)(128)(2,1)S(1)}, bf16[96]{0:T(256)(128)(2,1)S(1)}, bf16[96]{0:T(256)(128)(2,1)S(1)}, bf16[96]{0:T(256)(128)(2,1)S(1)}, bf16[9...) all-reduce(bf16[96]{0:T(256)(128)(2,1)S(1)} %dynamic-slice.43, ...), channel_id=1, replica_groups=mesh['seq'=4,'shard'=8] {'seq'}, use_global_device_ids=true, to_apply=%region_35.36 | all-reduce | flops 1152 | bytes 4608 | tf_op jit(solution)/shard_map/psum | solution.py:359
  863.6 30.5 %all-reduce.23.cloned.1.call-done = (bf16[96,2304]{0,1:T(8,128)(2,1)}, bf16[96,768]{1,0:T(8,128)(2,1)}, bf16[96,3072]{1,0:T(8,128)(2,1)}, bf16[384,768]{1,0:T(8,128)(2,1)}) async-done(((bf16[96,2304]{0,1:T(8,128)(2,1)}, bf16[96,768]{1,0:T(8,128)(2,1)}, bf16[96,3072]{1,0:T(8,128)(2,1)}, bf16[384,768]{1,0:T(8,128)(2,1)}), (bf16[96,2304]{0,1:T(8,128)(2,1)}, bf16[96,768]{1,0:T(8,128)(2,1)}, ...) | async-done | bytes 1769488 | tf_op jit(solution)/shard_map/psum | solution.py:358
  (455 shorter events, 476.7 us)
Async XLA Ops:
  7.2 39.5 %all-gather.6.cloned.1.call-start = ((), (), s32[]{:S(2)}) async-start(), calls=%async_computation.12 | async-start | bytes 3981312 | tf_op jit(solution)/shard_map/all_gather | solution.py:54
  57.0 59.0 %all-to-all-start = ((bf16[512,3,4,192]{0,3,1,2:T(8,128)(2,1)}), bf16[512,3,4,192]{0,3,1,2:T(8,128)(2,1)S(1)}, u32[]{:S(2)}, u32[]{:S(2)}) async-start(bf16[512,3,4,192]{0,3,1,2:T(8,128)(2,1)} %copy.83), calls=%async_computation | async-start | bytes 4718592 | tf_op jit(solution)/shard_map/all_to_all | solution.py:251
  61.7 181.3 %all-gather.8.cloned.1.call-start = ((), (), s32[]{:S(2)}) async-start(), calls=%async_computation.13 | async-start | bytes 1327104 | tf_op jit(solution)/shard_map/all_gather | solution.py:57
  62.4 192.6 %all-gather.10.cloned.1.call-start = ((), (), s32[]{:S(2)}) async-start(), calls=%async_computation.14 | async-start | bytes 5308416 | tf_op jit(solution)/shard_map/all_gather | solution.py:61
  115.9 58.1 %all-to-all-start.2 = ((bf16[512,3,4,192]{0,3,1,2:T(8,128)(2,1)}), bf16[512,3,4,192]{0,3,1,2:T(8,128)(2,1)}, u32[]{:S(2)}, u32[]{:S(2)}) async-start(bf16[512,3,4,192]{0,3,1,2:T(8,128)(2,1)} %copy.87), calls=%async_computation.2 | async-start | bytes 4718592 | tf_op jit(solution)/shard_map/all_to_all | solution.py:251
  169.6 13.9 %copy-start.11 = (bf16[2048,3,64]{0,2,1:T(8,128)(2,1)}, bf16[2048,3,64]{0,2,1:T(8,128)(2,1)S(1)}, u32[]{:S(2)}) copy-start(bf16[2048,3,64]{0,2,1:T(8,128)(2,1)S(1)} %get-tuple-element.1048) | copy-start | bytes 2359300
  169.6 13.9 %copy-start.14 = (bf16[4,512,3,64]{1,3,2,0:T(8,128)(2,1)}, bf16[4,512,3,64]{1,3,2,0:T(8,128)(2,1)S(1)}, u32[]{:S(2)}) copy-start(bf16[4,512,3,64]{1,3,2,0:T(8,128)(2,1)S(1)} %get-tuple-element.1053) | copy-start | bytes 2359300
  169.6 13.9 %copy-start.37 = (f32[4,3,512]{2,1,0:T(4,128)}, f32[4,3,512]{2,1,0:T(4,128)S(1)}, u32[]{:S(2)}) copy-start(f32[4,3,512]{2,1,0:T(4,128)S(1)} %get-tuple-element.995) | copy-start | bytes 73732
  174.1 52.1 %all-to-all-start.1 = ((bf16[4,512,192]{1,2,0:T(8,128)(2,1)}), bf16[4,512,192]{1,2,0:T(8,128)(2,1)}, u32[]{:S(2)}, u32[]{:S(2)}) async-start(bf16[4,512,192]{1,2,0:T(8,128)(2,1)} %bitcast.8), calls=%async_computation.1 | async-start | bytes 1572864 | tf_op jit(solution)/shard_map/all_to_all | solution.py:260
  192.0 40.6 %copy-start.63 = (bf16[768]{0:T(1024)(128)(2,1)S(1)}, bf16[768]{0:T(1024)(128)(2,1)}, u32[]{:S(2)}) copy-start(bf16[768]{0:T(1024)(128)(2,1)} %get-tuple-element.570) | copy-start | bytes 4612
  192.1 40.6 %copy-start.62 = (bf16[768]{0:T(1024)(128)(2,1)S(1)}, bf16[768]{0:T(1024)(128)(2,1)}, u32[]{:S(2)}) copy-start(bf16[768]{0:T(1024)(128)(2,1)} %get-tuple-element.572) | copy-start | bytes 4612
  192.1 40.6 %copy-start.61 = (bf16[768]{0:T(1024)(128)(2,1)S(1)}, bf16[768]{0:T(1024)(128)(2,1)}, u32[]{:S(2)}) copy-start(bf16[768]{0:T(1024)(128)(2,1)} %get-tuple-element.571) | copy-start | bytes 4612
  192.1 40.6 %copy-start.65 = (bf16[384]{0:T(512)(128)(2,1)S(1)}, bf16[384]{0:T(512)(128)(2,1)}, u32[]{:S(2)}) copy-start(bf16[384]{0:T(512)(128)(2,1)} %param.34) | copy-start | bytes 2308
  192.1 49.5 %copy-start.60 = (bf16[768]{0:T(1024)(128)(2,1)S(1)}, bf16[768]{0:T(1024)(128)(2,1)}, u32[]{:S(2)}) copy-start(bf16[768]{0:T(1024)(128)(2,1)} %get-tuple-element.573) | copy-start | bytes 4612
  192.1 49.5 %copy-start.59 = (bf16[768]{0:T(1024)(128)(2,1)S(1)}, bf16[768]{0:T(1024)(128)(2,1)}, u32[]{:S(2)}) copy-start(bf16[768]{0:T(1024)(128)(2,1)} %get-tuple-element.574) | copy-start | bytes 4612
  192.1 49.5 %copy-start.58 = (bf16[768]{0:T(1024)(128)(2,1)S(1)}, bf16[768]{0:T(1024)(128)(2,1)}, u32[]{:S(2)}) copy-start(bf16[768]{0:T(1024)(128)(2,1)} %get-tuple-element.575) | copy-start | bytes 4612
  226.1 20.7 %copy-start.4 = (bf16[2048,3,64]{0,2,1:T(8,128)(2,1)}, bf16[2048,3,64]{0,2,1:T(8,128)(2,1)S(1)}, u32[]{:S(2)}) copy-start(bf16[2048,3,64]{0,2,1:T(8,128)(2,1)S(1)} %get-tuple-element.1041) | copy-start | bytes 2359300
  226.1 20.7 %copy-start.9 = (bf16[2048,3,64]{0,2,1:T(8,128)(2,1)}, bf16[2048,3,64]{0,2,1:T(8,128)(2,1)S(1)}, u32[]{:S(2)}) copy-start(bf16[2048,3,64]{0,2,1:T(8,128)(2,1)S(1)} %get-tuple-element.1047) | copy-start | bytes 2359300
  226.1 20.7 %copy-start.13 = (bf16[4,512,3,64]{1,3,2,0:T(8,128)(2,1)}, bf16[4,512,3,64]{1,3,2,0:T(8,128)(2,1)S(1)}, u32[]{:S(2)}) copy-start(bf16[4,512,3,64]{1,3,2,0:T(8,128)(2,1)S(1)} %get-tuple-element.1052) | copy-start | bytes 2359300
  226.1 20.7 %copy-start.38 = (f32[4,3,512]{2,1,0:T(4,128)}, f32[4,3,512]{2,1,0:T(4,128)S(1)}, u32[]{:S(2)}) copy-start(f32[4,3,512]{2,1,0:T(4,128)S(1)} %get-tuple-element.959) | copy-start | bytes 73732
  227.0 24.2 %all-to-all-start.3 = ((bf16[4,512,192]{1,2,0:T(8,128)(2,1)}), bf16[4,512,192]{1,2,0:T(8,128)(2,1)S(1)}, u32[]{:S(2)}, u32[]{:S(2)}) async-start(bf16[4,512,192]{1,2,0:T(8,128)(2,1)} %bitcast.341), calls=%async_computation.3 | async-start | bytes 1572864 | tf_op jit(solution)/shard_map/all_to_all | solution.py:260
  232.0 65.4 %all-gather.12.cloned.1.call-start = ((), (), s32[]{:S(2)}) async-start(), calls=%async_computation.15 | async-start | bytes 5308416 | tf_op jit(solution)/shard_map/all_gather | solution.py:63
  232.6 516.5 %reduce-scatter.7.cloned.1.call-start = ((), (), s32[]{:S(2)}) async-start(), calls=%async_computation.16 | async-start | bytes 2654208 | tf_op jit(solution)/shard_map/reduce_scatter | solution.py:346
  359.8 393.6 %reduce-scatter.11.cloned.1.call-start = ((), (), s32[]{:S(2)}) async-start(), calls=%async_computation.18 | async-start | bytes 10616832 | tf_op jit(solution)/shard_map/reduce_scatter | solution.py:352
  375.6 26.2 %all-to-all-start.4 = ((bf16[512,4,192]{0,2,1:T(8,128)(2,1)}), bf16[512,4,192]{0,2,1:T(8,128)(2,1)}, u32[]{:S(2)}, u32[]{:S(2)}) async-start(bf16[512,4,192]{0,2,1:T(8,128)(2,1)} %bitcast.340), calls=%async_computation.4 | async-start | bytes 1572864 | tf_op jit(solution)/shard_map/all_to_all | solution.py:312
  379.8 376.0 %reduce-scatter.9.cloned.1.call-start = ((), (), s32[]{:S(2)}) async-start(), calls=%async_computation.17 | async-start | bytes 10616832 | tf_op jit(solution)/shard_map/reduce_scatter | solution.py:350
  401.8 137.0 %all-to-all-start.6 = ((bf16[512,4,192]{0,2,1:T(8,128)(2,1)}), bf16[512,4,192]{0,2,1:T(8,128)(2,1)}, u32[]{:S(2)}, u32[]{:S(2)}) async-start(bf16[512,4,192]{0,2,1:T(8,128)(2,1)} %bitcast.339), calls=%async_computation.6 | async-start | bytes 1572864 | tf_op jit(solution)/shard_map/all_to_all | solution.py:312
  538.8 134.0 %all-to-all-start.5 = ((bf16[4,512,3,1,192]{1,4,2,3,0:T(8,128)(2,1)}), bf16[4,512,3,1,192]{1,4,2,3,0:T(8,128)(2,1)}, u32[]{:S(2)}, u32[]{:S(2)}) async-start(bf16[4,512,3,1,192]{1,4,2,3,0:T(8,128)(2,1)} %pad_maximum_fusion.1), calls=%async_computation.5 | async-start | bytes 4718592 | tf_op jit(solution)/shard_map/all_to_all | solution.py:317
  672.7 54.1 %all-to-all-start.7 = ((bf16[4,512,3,1,192]{1,4,2,3,0:T(8,128)(2,1)}), bf16[4,512,3,1,192]{1,4,2,3,0:T(8,128)(2,1)S(1)}, u32[]{:S(2)}, u32[]{:S(2)}) async-start(bf16[4,512,3,1,192]{1,4,2,3,0:T(8,128)(2,1)} %pad_maximum_fusion.3), calls=%async_computation.7 | async-start | bytes 4718592 | tf_op jit(solution)/shard_map/all_to_all | solution.py:317
  677.8 131.4 %reduce-scatter.13.cloned.1.call-start = ((), (), s32[]{:S(2)}) async-start(), calls=%async_computation.19 | async-start | bytes 7962624
  745.0 149.1 %all-reduce.23.cloned.1.call-start = ((), (), s32[]{:S(2)}) async-start(), calls=%async_computation.20 | async-start | bytes 3833856 | tf_op jit(solution)/shard_map/psum | solution.py:358
  758.1 96.6 %copy-start.51 = (f32[512]{0:T(512)S(1)}, f32[512]{0:T(512)}, u32[]{:S(2)}) copy-start(f32[512]{0:T(512)} %copy-done.50) | copy-start | bytes 6148
  (70 other events, 359.1 us)
Sparse Core Ops, SparseCore 0:
  9.9 36.7 all-gather.5
  64.4 24.3 all-gather.7
  90.7 38.7 all-gather.9
  234.4 39.2 all-gather.11
  359.9 40.3 reduce-scatter.6
  403.7 76.8 reduce-scatter.10
  484.1 76.8 reduce-scatter.8
  745.1 63.9 reduce-scatter.12
  812.9 81.1 all-reduce.22
